TPU v7x, 32 devices: a whole 2x2x4 slice. The times are simulated.
32 devices in a mesh: gy: 4 (over z), gz: 8 (over y, x, core).
Axes of the slice: x: 2, y: 2, z: 4, core: 2. Of those that a mesh axis runs over, the one named last changes fastest.
Arguments:
- data_weight: float32 [320, 160, 640], P('gy', 'gz'), may hold values from 0.25 to 4
- blob_taps: float32 [3, 7], replicated, may hold values from 0.2 to 1
Outputs:
- new_weight: float32 [320, 160, 640], P('gy', 'gz')
- changes: float32 [3], replicated
All inputs are finite; a program needn't handle non-finite values.
Results may differ from a plain program's by a relative error of at most 0.00002.
Values sent between devices are 32-bit elements; how exact they have to be, the bound alone decides.
A program may use at most 64 MiB of HBM per device.

v0:
```python
import jax
import jax.numpy as jnp
from jax import lax
from jax.sharding import PartitionSpec as P

RAD = 3
ITERS = 3


def with_halo(cells, sides, width):
    for axis, dim in sides:
        count = lax.axis_size(axis)
        ends = count - 1
        head = lax.slice_in_dim(cells, 0, width, axis=dim)
        tail = lax.slice_in_dim(cells, cells.shape[dim] - width, cells.shape[dim], axis=dim)
        cells = jnp.concatenate(
            [
                lax.ppermute(tail, axis, [(i, (i + 1) % count) for i in range(ends)]),
                cells,
                lax.ppermute(head, axis, [((i + 1) % count, i) for i in range(ends)]),
            ],
            axis=dim,
        )
    return cells


def smear_valid(padded, kernel, axis_dim):
    length = padded.shape[axis_dim] - 2 * RAD
    result = kernel[0] * lax.slice_in_dim(padded, 0, length, axis=axis_dim)
    for offset in range(1, 2 * RAD + 1):
        result = result + kernel[offset] * lax.slice_in_dim(
            padded, offset, offset + length, axis=axis_dim
        )
    return result


def smear_local(field, kernel):
    padded = jnp.pad(field, ((0, 0), (0, 0), (RAD, RAD)))
    return smear_valid(padded, kernel, 2)


def shards(data_weight, blob_taps):
    kernel = blob_taps / jnp.sum(blob_taps, axis=1, keepdims=True)
    changes = []
    weight = jnp.ones_like(data_weight)
    for iteration in range(ITERS):
        product = weight * data_weight
        blurred = smear_local(product, kernel[2])
        padded = with_halo(blurred, (("gy", 0),), RAD)
        blurred = smear_valid(padded, kernel[0], 0)
        padded = with_halo(blurred, (("gz", 1),), RAD)
        blurred = smear_valid(padded, kernel[1], 1)
        weight = weight / blurred
        deviation = jnp.max(jnp.abs(blurred - 1.0))
        changes.append(lax.pmax(deviation, ("gy", "gz")))
    result_max = jnp.stack(changes)
    return (weight, result_max)


def solution(mesh):
    return jax.shard_map(
        shards,
        mesh=mesh,
        in_specs=(P("gy", "gz", None), P()),
        out_specs=(P("gy", "gz", None), P()),
        check_vma=False,
    )
```

profile of v0, /device:TPU:0, one launch (start us, length us, event | category | flops | bytes accessed | tf_op | source)
XLA Modules:
  0.0 279.0 jit_solution(5993323312113206324)
XLA Ops:
  3.4 21.3 %fusion.90 = f32[80,20,640]{2,0,1:T(8,128)S(1)} fusion(f32[80,20,640]{2,0,1:T(8,128)} %param.2, f32[]{:T(128)} %bitcast.8, f32[]{:T(128)} %bitcast.7, f32[]{:T(128)} %bitcast.6, f32[]{:T(128)} %bitcast.5, f32[]{:T(128)} %bitcast.4, f32[]{:T(128)} %bitcast.3, f32[]{:T(128)} %bitcast.2), kind=kLoop, calls=%fused_computation.156 | loop fusion | flops 13312000 | bytes 8192028 | tf_op jit(solution)/shard_map/add | solution.py:31
  24.8 5.0 %collective-permute-start = (f32[3,20,640]{2,0,1:T(4,128)S(1)}, f32[3,20,640]{2,0,1:T(4,128)S(1)}, u32[]{:S(2)}, u32[]{:S(2)}) collective-permute-start(f32[3,20,640]{2,0,1:T(4,128)S(1)} %get-tuple-element.23), channel_id=1, source_target_pairs={{0,8},{8,16},{16,24},{1,9},{9,17},{17,25},{2,10},{10,18},{18,26},{... | collective-permute-start | bytes 460808 | tf_op jit(solution)/shard_map/ppermute | solution.py:18
  29.8 1.3 collective-permute-start.1
  31.1 3.0 %collective-permute-done = f32[3,20,640]{2,0,1:T(4,128)S(1)} collective-permute-done((f32[3,20,640]{2,0,1:T(4,128)S(1)}, f32[3,20,640]{2,0,1:T(4,128)S(1)}, u32[]{:S(2)}, u32[]{:S(2)}) %collective-permute-start) | collective-permute-done | bytes 153632 | tf_op jit(solution)/shard_map/ppermute | solution.py:18
  34.1 4.1 %collective-permute-done.1 = f32[3,20,640]{2,0,1:T(4,128)S(1)} collective-permute-done((f32[3,20,640]{2,0,1:T(4,128)S(1)}, f32[3,20,640]{2,0,1:T(4,128)S(1)}, u32[]{:S(2)}, u32[]{:S(2)}) %collective-permute-start.1) | collective-permute-done | bytes 153632 | tf_op jit(solution)/shard_map/ppermute | solution.py:20
  38.2 8.2 %fusion.31 = f32[80,20,640]{2,0,1:T(8,128)S(1)} fusion(f32[80,20,640]{2,0,1:T(8,128)S(1)} %fusion.90, f32[3,20,640]{2,0,1:T(4,128)S(1)} %collective-permute-done.1, f32[3,20,640]{2,0,1:T(4,128)S(1)} %collective-permute-done, f32[]{:T(128)} %bitcast.14, f32[]{:T(128)} %bitcast.13, f32[]{:T(128)} %bitcast.12, f32[]{:T(128)} %bitcast.11, f32[]{:T(128)} %bitcast.10, ...), kind=kLoop, calls=%fused_computation.97 | loop fusion | flops 19456000 | bytes 8499228 | tf_op jit(solution)/shard_map/add | solution.py:31
  46.5 1.3 collective-permute-start.2
  49.5 4.0 %collective-permute-done.3 = f32[80,3,640]{2,0,1:T(8,128)S(1)} collective-permute-done((f32[80,3,640]{2,0,1:T(8,128)S(1)}, f32[80,3,640]{2,0,1:T(8,128)S(1)}, u32[]{:S(2)}, u32[]{:S(2)}) %collective-permute-start.3) | collective-permute-done | bytes 614432 | tf_op jit(solution)/shard_map/ppermute | solution.py:20
  53.5 16.5 %abs_reduce_fusion.2 = (f32[]{:T(128)}, f32[80,20,640]{2,0,1:T(8,128)S(1)}) fusion(f32[80,3,640]{2,0,1:T(8,128)S(1)} %collective-permute-done.3, f32[80,20,640]{2,0,1:T(8,128)} %copy-done.1, f32[]{:T(128)} %bitcast.20, f32[]{:T(128)} %bitcast.19, f32[]{:T(128)} %bitcast.18, f32[]{:T(128)} %bitcast.17, f32[80,3,640]{2,0,1:T(8,128)S(1)} %collective-permute-done.2, ...), kind=kLoop, calls=%fused_computation.212 | loop fusion | flops 22528000 | bytes 9420832 | tf_op jit(solution)/shard_map/reduce_max | solution.py:54
  70.0 2.5 divide_multiply_fusion.1
  72.5 21.1 %fusion.102 = f32[80,20,640]{2,0,1:T(8,128)S(1)} fusion(f32[80,20,640]{2,0,1:T(8,128)} %divide_multiply_fusion.1, f32[]{:T(128)} %bitcast.8, f32[]{:T(128)} %bitcast.7, f32[]{:T(128)} %bitcast.6, f32[]{:T(128)} %bitcast.5, f32[]{:T(128)} %bitcast.4, f32[]{:T(128)} %bitcast.3, f32[]{:T(128)} %bitcast.2), kind=kLoop, calls=%fused_computation.168 | loop fusion | flops 13312000 | bytes 8192028 | tf_op jit(solution)/shard_map/add | solution.py:31
  93.7 3.5 %collective-permute-start.4 = (f32[3,20,640]{2,0,1:T(4,128)S(1)}, f32[3,20,640]{2,0,1:T(4,128)S(1)}, u32[]{:S(2)}, u32[]{:S(2)}) collective-permute-start(f32[3,20,640]{2,0,1:T(4,128)S(1)} %get-tuple-element.19), channel_id=1, source_target_pairs={{0,8},{8,16},{16,24},{1,9},{9,17},{17,25},{2,10},{10,18},{18,26},{... | collective-permute-start | bytes 460808 | tf_op jit(solution)/shard_map/ppermute | solution.py:18
  98.5 1.9 collective-permute-done.4
  100.4 4.4 %collective-permute-done.5 = f32[3,20,640]{2,0,1:T(4,128)S(1)} collective-permute-done((f32[3,20,640]{2,0,1:T(4,128)S(1)}, f32[3,20,640]{2,0,1:T(4,128)S(1)}, u32[]{:S(2)}, u32[]{:S(2)}) %collective-permute-start.5) | collective-permute-done | bytes 153632 | tf_op jit(solution)/shard_map/ppermute | solution.py:20
  104.8 8.2 %fusion.17 = f32[80,20,640]{2,0,1:T(8,128)S(1)} fusion(f32[80,20,640]{2,0,1:T(8,128)S(1)} %fusion.102, f32[3,20,640]{2,0,1:T(4,128)S(1)} %collective-permute-done.5, f32[3,20,640]{2,0,1:T(4,128)S(1)} %collective-permute-done.4, f32[]{:T(128)} %bitcast.14, f32[]{:T(128)} %bitcast.13, f32[]{:T(128)} %bitcast.12, f32[]{:T(128)} %bitcast.11, f32[]{:T(128)} %bitcast.10, ...), kind=kLoop, calls=%fused_computation.83 | loop fusion | flops 19456000 | bytes 8499228 | tf_op jit(solution)/shard_map/add | solution.py:31
  113.1 2.0 copy-done.2
  115.1 12.6 %collective-permute-start.6 = (f32[80,3,640]{2,0,1:T(8,128)S(1)}, f32[80,3,640]{2,0,1:T(8,128)S(1)}, u32[]{:S(2)}, u32[]{:S(2)}) collective-permute-start(f32[80,3,640]{2,0,1:T(8,128)S(1)} %get-tuple-element.17), channel_id=1, source_target_pairs={{0,1},{1,2},{2,3},{3,4},{4,5},{5,6},{6,7},{8,9},{9,10},{10,11},{11... | collective-permute-start | bytes 1843208 | tf_op jit(solution)/shard_map/ppermute | solution.py:18
  129.3 4.7 %collective-permute-done.7 = f32[80,3,640]{2,0,1:T(8,128)S(1)} collective-permute-done((f32[80,3,640]{2,0,1:T(8,128)S(1)}, f32[80,3,640]{2,0,1:T(8,128)S(1)}, u32[]{:S(2)}, u32[]{:S(2)}) %collective-permute-start.7) | collective-permute-done | bytes 614432 | tf_op jit(solution)/shard_map/ppermute | solution.py:20
  134.0 17.7 %abs_reduce_fusion.1 = (f32[]{:T(128)}, f32[80,20,640]{2,0,1:T(8,128)}) fusion(f32[80,3,640]{2,0,1:T(8,128)S(1)} %collective-permute-done.7, f32[80,20,640]{2,0,1:T(8,128)} %copy-done.2, f32[]{:T(128)} %bitcast.20, f32[]{:T(128)} %bitcast.19, f32[]{:T(128)} %bitcast.18, f32[]{:T(128)} %bitcast.17, f32[80,3,640]{2,0,1:T(8,128)S(1)} %collective-permute-done.6, ...), kind=kLoop, calls=%fused_computation.211 | loop fusion | flops 22528000 | bytes 9420832 | tf_op jit(solution)/shard_map/reduce_max | solution.py:54
  151.7 6.3 %divide_multiply_fusion = (f32[80,20,640]{2,0,1:T(8,128)}, f32[80,20,640]{2,0,1:T(8,128)}) fusion(f32[80,20,640]{2,0,1:T(8,128)S(1)} %copy-done, f32[80,20,640]{2,0,1:T(8,128)S(1)} %get-tuple-element.6, f32[80,20,640]{2,0,1:T(8,128)} %get-tuple-element.8), kind=kLoop, calls=%fused_computation.214 | loop fusion | flops 3072000 | bytes 20480000 | tf_op jit(solution)/shard_map/mul | solution.py:47
  158.0 21.1 %fusion.114 = f32[80,20,640]{2,0,1:T(8,128)S(1)} fusion(f32[80,20,640]{2,0,1:T(8,128)} %get-tuple-element.11, f32[]{:T(128)} %bitcast.8, f32[]{:T(128)} %bitcast.7, f32[]{:T(128)} %bitcast.6, f32[]{:T(128)} %bitcast.5, f32[]{:T(128)} %bitcast.4, f32[]{:T(128)} %bitcast.3, f32[]{:T(128)} %bitcast.2), kind=kLoop, calls=%fused_computation.180 | loop fusion | flops 13312000 | bytes 8192028 | tf_op jit(solution)/shard_map/add | solution.py:31
  179.1 3.5 %collective-permute-start.8 = (f32[3,20,640]{2,0,1:T(4,128)S(1)}, f32[3,20,640]{2,0,1:T(4,128)S(1)}, u32[]{:S(2)}, u32[]{:S(2)}) collective-permute-start(f32[3,20,640]{2,0,1:T(4,128)S(1)} %get-tuple-element.15), channel_id=1, source_target_pairs={{0,8},{8,16},{16,24},{1,9},{9,17},{17,25},{2,10},{10,18},{18,26},{... | collective-permute-start | bytes 460808 | tf_op jit(solution)/shard_map/ppermute | solution.py:18
  183.9 1.9 collective-permute-done.8
  185.9 4.4 %collective-permute-done.9 = f32[3,20,640]{2,0,1:T(4,128)S(1)} collective-permute-done((f32[3,20,640]{2,0,1:T(4,128)S(1)}, f32[3,20,640]{2,0,1:T(4,128)S(1)}, u32[]{:S(2)}, u32[]{:S(2)}) %collective-permute-start.9) | collective-permute-done | bytes 153632 | tf_op jit(solution)/shard_map/ppermute | solution.py:20
  190.3 8.2 %fusion.3 = f32[80,20,640]{2,0,1:T(8,128)S(1)} fusion(f32[80,20,640]{2,0,1:T(8,128)S(1)} %fusion.114, f32[3,20,640]{2,0,1:T(4,128)S(1)} %collective-permute-done.9, f32[3,20,640]{2,0,1:T(4,128)S(1)} %collective-permute-done.8, f32[]{:T(128)} %bitcast.14, f32[]{:T(128)} %bitcast.13, f32[]{:T(128)} %bitcast.12, f32[]{:T(128)} %bitcast.11, f32[]{:T(128)} %bitcast.10, ...), kind=kLoop, calls=%fused_computation.69 | loop fusion | flops 19456000 | bytes 8499228 | tf_op jit(solution)/shard_map/add | solution.py:31
  198.6 11.1 %collective-permute-start.10 = (f32[80,3,640]{2,0,1:T(8,128)S(1)}, f32[80,3,640]{2,0,1:T(8,128)S(1)}, u32[]{:S(2)}, u32[]{:S(2)}) collective-permute-start(f32[80,3,640]{2,0,1:T(8,128)S(1)} %get-tuple-element.13), channel_id=1, source_target_pairs={{0,1},{1,2},{2,3},{3,4},{4,5},{5,6},{6,7},{8,9},{9,10},{10,11},{11... | collective-permute-start | bytes 1843208 | tf_op jit(solution)/shard_map/ppermute | solution.py:18
  209.8 1.6 collective-permute-start.11
  211.4 3.3 %collective-permute-done.11 = f32[80,3,640]{2,0,1:T(8,128)S(1)} collective-permute-done((f32[80,3,640]{2,0,1:T(8,128)S(1)}, f32[80,3,640]{2,0,1:T(8,128)S(1)}, u32[]{:S(2)}, u32[]{:S(2)}) %collective-permute-start.11) | collective-permute-done | bytes 614432 | tf_op jit(solution)/shard_map/ppermute | solution.py:20
  214.7 11.4 %abs_reduce_fusion = (f32[]{:T(128)}, f32[80,20,640]{2,0,1:T(8,128)}) fusion(f32[80,3,640]{2,0,1:T(8,128)S(1)} %collective-permute-done.11, f32[80,20,640]{2,0,1:T(8,128)S(1)} %fusion.3, f32[]{:T(128)} %bitcast.20, f32[]{:T(128)} %bitcast.19, f32[]{:T(128)} %bitcast.18, f32[]{:T(128)} %bitcast.17, f32[80,3,640]{2,0,1:T(8,128)S(1)} %collective-permute-done.10, ...), kind=kLoop, calls=%fused_computation.210 | loop fusion | flops 22528000 | bytes 9420832 | tf_op jit(solution)/shard_map/reduce_max | solution.py:54
  226.1 4.7 %multiply_divide_fusion = f32[80,20,640]{2,0,1:T(8,128)} fusion(f32[80,20,640]{2,0,1:T(8,128)S(1)} %copy-done.3, f32[80,20,640]{2,0,1:T(8,128)} %get-tuple-element.10), kind=kLoop, calls=%fused_computation.213 | loop fusion | flops 2048000 | bytes 12288000 | tf_op jit(solution)/shard_map/div | solution.py:53
  230.8 45.7 %all-reduce.3 = (f32[1]{0:T(128)}, f32[1]{0:T(128)}, f32[1]{0:T(128)}) all-reduce(f32[1]{0:T(128)} %bitcast.23, f32[1]{0:T(128)} %bitcast.22, f32[1]{0:T(128)} %bitcast.21), channel_id=1, replica_groups=mesh['gy'=4,'gz'=8] {'gy','gz'}, use_global_device_ids=true, to_apply=%region_6.7 | all-reduce | flops 3 | bytes 24 | tf_op jit(solution)/shard_map/pmax | solution.py:55
  276.5 2.5 pad_maximum_fusion.12
  (24 shorter events, 9.1 us)
Async XLA Ops:
  24.8 9.3 %collective-permute-start = (f32[3,20,640]{2,0,1:T(4,128)S(1)}, f32[3,20,640]{2,0,1:T(4,128)S(1)}, u32[]{:S(2)}, u32[]{:S(2)}) collective-permute-start(f32[3,20,640]{2,0,1:T(4,128)S(1)} %get-tuple-element.23), channel_id=1, source_target_pairs={{0,8},{8,16},{16,24},{1,9},{9,17},{17,25},{2,10},{10,18},{18,26},{... | collective-permute-start | bytes 460808 | tf_op jit(solution)/shard_map/ppermute | solution.py:18
  29.8 8.4 %collective-permute-start.1 = (f32[3,20,640]{2,0,1:T(4,128)S(1)}, f32[3,20,640]{2,0,1:T(4,128)S(1)}, u32[]{:S(2)}, u32[]{:S(2)}) collective-permute-start(f32[3,20,640]{2,0,1:T(4,128)S(1)} %get-tuple-element.24), channel_id=1, source_target_pairs={{8,0},{16,8},{24,16},{9,1},{17,9},{25,17},{10,2},{18,10},{26,18},{... | collective-permute-start | bytes 460808 | tf_op jit(solution)/shard_map/ppermute | solution.py:20
  46.4 7.1 %copy-start.1 = (f32[80,20,640]{2,0,1:T(8,128)}, f32[80,20,640]{2,0,1:T(8,128)S(1)}, u32[]{:S(2)}) copy-start(f32[80,20,640]{2,0,1:T(8,128)S(1)} %fusion.31) | copy-start | bytes 12288004
  46.5 2.9 %collective-permute-start.2 = (f32[80,3,640]{2,0,1:T(8,128)S(1)}, f32[80,3,640]{2,0,1:T(8,128)S(1)}, u32[]{:S(2)}, u32[]{:S(2)}) collective-permute-start(f32[80,3,640]{2,0,1:T(8,128)S(1)} %get-tuple-element.21), channel_id=1, source_target_pairs={{0,1},{1,2},{2,3},{3,4},{4,5},{5,6},{6,7},{8,9},{9,10},{10,11},{11... | collective-permute-start | bytes 1843208 | tf_op jit(solution)/shard_map/ppermute | solution.py:18
  47.8 5.6 %collective-permute-start.3 = (f32[80,3,640]{2,0,1:T(8,128)S(1)}, f32[80,3,640]{2,0,1:T(8,128)S(1)}, u32[]{:S(2)}, u32[]{:S(2)}) collective-permute-start(f32[80,3,640]{2,0,1:T(8,128)S(1)} %get-tuple-element.22), channel_id=1, source_target_pairs={{1,0},{2,1},{3,2},{4,3},{5,4},{6,5},{7,6},{9,8},{10,9},{11,10},{12... | collective-permute-start | bytes 1843208 | tf_op jit(solution)/shard_map/ppermute | solution.py:20
  53.5 16.5 %copy-start = (f32[80,20,640]{2,0,1:T(8,128)S(1)}, f32[80,20,640]{2,0,1:T(8,128)}, u32[]{:S(2)}) copy-start(f32[80,20,640]{2,0,1:T(8,128)} %param.2) | copy-start | bytes 12288004
  93.7 6.7 %collective-permute-start.4 = (f32[3,20,640]{2,0,1:T(4,128)S(1)}, f32[3,20,640]{2,0,1:T(4,128)S(1)}, u32[]{:S(2)}, u32[]{:S(2)}) collective-permute-start(f32[3,20,640]{2,0,1:T(4,128)S(1)} %get-tuple-element.19), channel_id=1, source_target_pairs={{0,8},{8,16},{16,24},{1,9},{9,17},{17,25},{2,10},{10,18},{18,26},{... | collective-permute-start | bytes 460808 | tf_op jit(solution)/shard_map/ppermute | solution.py:18
  97.2 7.7 %collective-permute-start.5 = (f32[3,20,640]{2,0,1:T(4,128)S(1)}, f32[3,20,640]{2,0,1:T(4,128)S(1)}, u32[]{:S(2)}, u32[]{:S(2)}) collective-permute-start(f32[3,20,640]{2,0,1:T(4,128)S(1)} %get-tuple-element.20), channel_id=1, source_target_pairs={{8,0},{16,8},{24,16},{9,1},{17,9},{25,17},{10,2},{18,10},{26,18},{... | collective-permute-start | bytes 460808 | tf_op jit(solution)/shard_map/ppermute | solution.py:20
  113.1 2.0 copy-start.2
  115.1 14.2 %collective-permute-start.6 = (f32[80,3,640]{2,0,1:T(8,128)S(1)}, f32[80,3,640]{2,0,1:T(8,128)S(1)}, u32[]{:S(2)}, u32[]{:S(2)}) collective-permute-start(f32[80,3,640]{2,0,1:T(8,128)S(1)} %get-tuple-element.17), channel_id=1, source_target_pairs={{0,1},{1,2},{2,3},{3,4},{4,5},{5,6},{6,7},{8,9},{9,10},{10,11},{11... | collective-permute-start | bytes 1843208 | tf_op jit(solution)/shard_map/ppermute | solution.py:18
  127.7 6.3 %collective-permute-start.7 = (f32[80,3,640]{2,0,1:T(8,128)S(1)}, f32[80,3,640]{2,0,1:T(8,128)S(1)}, u32[]{:S(2)}, u32[]{:S(2)}) collective-permute-start(f32[80,3,640]{2,0,1:T(8,128)S(1)} %get-tuple-element.18), channel_id=1, source_target_pairs={{1,0},{2,1},{3,2},{4,3},{5,4},{6,5},{7,6},{9,8},{10,9},{11,10},{12... | collective-permute-start | bytes 1843208 | tf_op jit(solution)/shard_map/ppermute | solution.py:20
  179.1 6.7 %collective-permute-start.8 = (f32[3,20,640]{2,0,1:T(4,128)S(1)}, f32[3,20,640]{2,0,1:T(4,128)S(1)}, u32[]{:S(2)}, u32[]{:S(2)}) collective-permute-start(f32[3,20,640]{2,0,1:T(4,128)S(1)} %get-tuple-element.15), channel_id=1, source_target_pairs={{0,8},{8,16},{16,24},{1,9},{9,17},{17,25},{2,10},{10,18},{18,26},{... | collective-permute-start | bytes 460808 | tf_op jit(solution)/shard_map/ppermute | solution.py:18
  182.6 7.7 %collective-permute-start.9 = (f32[3,20,640]{2,0,1:T(4,128)S(1)}, f32[3,20,640]{2,0,1:T(4,128)S(1)}, u32[]{:S(2)}, u32[]{:S(2)}) collective-permute-start(f32[3,20,640]{2,0,1:T(4,128)S(1)} %get-tuple-element.16), channel_id=1, source_target_pairs={{8,0},{16,8},{24,16},{9,1},{17,9},{25,17},{10,2},{18,10},{26,18},{... | collective-permute-start | bytes 460808 | tf_op jit(solution)/shard_map/ppermute | solution.py:20
  198.6 12.7 %collective-permute-start.10 = (f32[80,3,640]{2,0,1:T(8,128)S(1)}, f32[80,3,640]{2,0,1:T(8,128)S(1)}, u32[]{:S(2)}, u32[]{:S(2)}) collective-permute-start(f32[80,3,640]{2,0,1:T(8,128)S(1)} %get-tuple-element.13), channel_id=1, source_target_pairs={{0,1},{1,2},{2,3},{3,4},{4,5},{5,6},{6,7},{8,9},{9,10},{10,11},{11... | collective-permute-start | bytes 1843208 | tf_op jit(solution)/shard_map/ppermute | solution.py:18
  209.7 16.4 %copy-start.3 = (f32[80,20,640]{2,0,1:T(8,128)S(1)}, f32[80,20,640]{2,0,1:T(8,128)}, u32[]{:S(2)}) copy-start(f32[80,20,640]{2,0,1:T(8,128)} %get-tuple-element.12) | copy-start | bytes 12288004
  209.8 4.9 %collective-permute-start.11 = (f32[80,3,640]{2,0,1:T(8,128)S(1)}, f32[80,3,640]{2,0,1:T(8,128)S(1)}, u32[]{:S(2)}, u32[]{:S(2)}) collective-permute-start(f32[80,3,640]{2,0,1:T(8,128)S(1)} %get-tuple-element.14), channel_id=1, source_target_pairs={{1,0},{2,1},{3,2},{4,3},{5,4},{6,5},{7,6},{9,8},{10,9},{11,10},{12... | collective-permute-start | bytes 1843208 | tf_op jit(solution)/shard_map/ppermute | solution.py:20
where the time goes:
time: 280 us; the launch traced here: 279 us
  other arithmetic  151 us (54%)
  blocking collectives  45.7 us (16%)
  starting transfers between devices  45 us (16%)
  waiting for transfers between devices  32.6 us (12%)
  local copies, waits for them, and re-layouts  3.7 us (1%)
    add x6, other arithmetic, smear_valid(): result + kernel[offset] * lax.slice_in_dim(padded, offset, offset + lengt...  88 us
    pmax x1, blocking collectives, shards(): changes.append(lax.pmax(deviation, ('gy', 'gz')))  45.7 us
    reduce_max x3, other arithmetic, shards(): deviation = jnp.max(jnp.abs(blurred - 1.0))  45.7 us
    ppermute x6, starting transfers between devices, with_halo(): lax.ppermute(tail, axis, [(i, (i + 1) % count) for i in range(ends)])  37 us
    ppermute x6, waiting for transfers between devices, with_halo(): lax.ppermute(head, axis, [((i + 1) % count, i) for i in range(ends)])  25 us
    mul x2, other arithmetic, shards(): product = weight * data_weight  8.77 us
    ppermute x6, starting transfers between devices, with_halo(): lax.ppermute(head, axis, [((i + 1) % count, i) for i in range(ends)])  8.02 us
    ppermute x6, waiting for transfers between devices, with_halo(): lax.ppermute(tail, axis, [(i, (i + 1) % count) for i in range(ends)])  7.55 us
  transfers between devices with their start and end apart: 12, of which 11 were waited for; matrix products, arithmetic and copies ran while one was open for 0% of the time, Pallas kernels for 0%

commit v1 on v0

v1 whole, which is shorter than its diff:
```python
import functools

import jax
import jax.numpy as jnp
from jax import lax
from jax.experimental import pallas as pl
from jax.experimental.pallas import tpu as pltpu
from jax.sharding import PartitionSpec as P

RAD = 3
ITERS = 3
TAPS = 2 * RAD + 1
LANES = 128
PAD = 8


def body(
    taps_ref, d_hbm, o_hbm, c_ref,
    D, W, Q, T, S, ZR, YSB, YRB, YSI, YRI, M, CS, CR1, CR2,
    in_sem, out_sem, zs, zr, ysb, yrb, ysi, yri, cs1, cr1, cs2, cr2,
):
    ny, nz, xlen = d_hbm.shape
    nb = xlen // LANES
    n_in = nz - 2 * RAD
    gy_n, gz_n = lax.axis_size("gy"), lax.axis_size("gz")
    gy, gz = lax.axis_index("gy"), lax.axis_index("gz")
    y_has = (gy > 0, gy < gy_n - 1)
    z_has = (gz > 0, gz < gz_n - 1)
    step = 16 if ny % 16 == 0 else 8

    barrier = pltpu.get_barrier_semaphore()
    for off in range(1, gy_n):
        pl.semaphore_signal(barrier, inc=1, device_id={"gy": lax.rem(gy + off, gy_n)})
    for off in range(1, gz_n):
        pl.semaphore_signal(barrier, inc=1, device_id={"gz": lax.rem(gz + off, gz_n)})

    edge_planes = list(range(RAD)) + list(range(nz - RAD, nz))
    inner_planes = list(range(RAD, nz - RAD))

    def in_copy(z, b):
        return pltpu.make_async_copy(
            d_hbm.at[:, z, pl.ds(b * LANES, LANES)], D.at[z, b + 1], in_sem.at[z, b]
        )

    def out_copy(z, b):
        return pltpu.make_async_copy(
            W.at[z, b], o_hbm.at[:, z, pl.ds(b * LANES, LANES)], out_sem.at[z, b]
        )

    for b in range(nb):
        for z in edge_planes:
            in_copy(z, b).start()
    for b in range(nb):
        for z in inner_planes:
            in_copy(z, b).start()

    blank = jnp.zeros((ny, LANES), jnp.float32)

    @pl.loop(0, nz)
    def _(z):
        for ref in (D, Q):
            ref[z, 0] = blank
            ref[z, nb + 1] = blank

    for side in range(2):
        @pl.when(jnp.logical_not(z_has[side]))
        def _():
            @pl.loop(0, ITERS * RAD)
            def _(i):
                for b in range(nb):
                    ZR[i // RAD, side, lax.rem(i, RAD), b] = blank

        @pl.when(jnp.logical_not(y_has[side]))
        def _():
            for it in range(ITERS):
                YRB[it, side] = jnp.zeros(YRB.shape[2:], jnp.float32)
                YRI[it, side] = jnp.zeros(YRI.shape[2:], jnp.float32)

    M[...] = jnp.zeros(M.shape, jnp.float32)
    CS[...] = jnp.zeros(CS.shape, jnp.float32)

    def tap_row(row):
        total = taps_ref[row, 0]
        for k in range(1, TAPS):
            total = total + taps_ref[row, k]
        bottom = jnp.full((8, LANES), total, jnp.float32)
        return [jnp.full((8, LANES), taps_ref[row, k], jnp.float32) / bottom for k in range(TAPS)]

    taps_y, taps_z, taps_x = tap_row(0), tap_row(1), tap_row(2)

    def wide(tap, rows):
        return tap if rows == 8 else jnp.concatenate([tap] * (rows // 8), axis=0)

    lane = lax.broadcasted_iota(jnp.int32, (step, LANES), 1)

    def plane_of(i):
        return i + (i // RAD) * n_in

    def smear_x(src, it, b, edge):
        kx = [wide(t, step) for t in taps_x]

        @pl.loop(0, 2 * RAD if edge else n_in)
        def _(i):
            z = plane_of(i) if edge else i + RAD
            for r in range(0, ny, step):
                rows = pl.ds(r, step)
                mid = src[z, b + 1, rows, :]
                left = src[z, b, rows, :]
                right = src[z, b + 2, rows, :]
                total = kx[RAD] * mid
                for s in range(1, RAD + 1):
                    up = pltpu.roll(jnp.where(lane < s, right, mid), LANES - s, 1)
                    down = pltpu.roll(jnp.where(lane >= LANES - s, left, mid), s, 1)
                    total = total + kx[RAD + s] * up + kx[RAD - s] * down
                T[z, b, pl.ds(PAD + r, step), :] = total
                send = YSB if edge else YSI
                if r == 0:
                    send[it, 0, b, i] = total[:RAD]
                if r + step == ny:
                    send[it, 1, b, i] = total[step - RAD:]

    def y_copy(it, to, b, edge):
        if edge:
            src, dst = YSB.at[it, to, b], YRB.at[it, 1 - to, b]
            ss, rs = ysb.at[it, to, b], yrb.at[it, 1 - to, b]
        else:
            src, dst = YSI.at[it, to], YRI.at[it, 1 - to]
            ss, rs = ysi.at[it, to], yri.at[it, 1 - to]
        peer = jnp.clip(gy + (1 if to else -1), 0, gy_n - 1)
        return pltpu.make_async_remote_copy(
            src_ref=src, dst_ref=dst, send_sem=ss, recv_sem=rs, device_id={"gy": peer}
        )

    def z_copy(it, to, b):
        first = nz - RAD if to else 0
        peer = jnp.clip(gz + (1 if to else -1), 0, gz_n - 1)
        return pltpu.make_async_remote_copy(
            src_ref=S.at[it, pl.ds(first, RAD), b],
            dst_ref=ZR.at[it, 1 - to, :, b],
            send_sem=zs.at[it, to, b],
            recv_sem=zr.at[it, 1 - to, b],
            device_id={"gz": peer},
        )

    def start(copy, has, *args):
        for to in range(2):
            @pl.when(has[to])
            def _():
                copy(args[0], to, *args[1:]).start()

    def arrived(copy, has, *args):
        for to in range(2):
            @pl.when(has[1 - to])
            def _():
                copy(args[0], to, *args[1:]).wait_recv()

    def sent(copy, has, *args):
        for to in range(2):
            @pl.when(has[to])
            def _():
                copy(args[0], to, *args[1:]).wait_send()

    def smear_y(it, b, edge):
        got = YRB if edge else YRI
        ky = [wide(t, step) for t in taps_y]

        @pl.loop(0, 2 * RAD if edge else n_in)
        def _(i):
            z = plane_of(i) if edge else i + RAD
            T[z, b, pl.ds(PAD - RAD, RAD), :] = got[it, 0, b, i]
            T[z, b, pl.ds(PAD + ny, RAD), :] = got[it, 1, b, i]
            for r in range(0, ny, step):
                total = ky[0] * T[z, b, pl.ds(PAD - RAD + r, step), :]
                for k in range(1, TAPS):
                    total = total + ky[k] * T[z, b, pl.ds(PAD - RAD + r + k, step), :]
                S[it, z, b, pl.ds(r, step), :] = total

    def smear_z(it, b, planes):
        kz = taps_z

        @pl.loop(0, ny // 8)
        def _(j):
            rows = pl.ds(pl.multiple_of(j * 8, 8), 8)
            needed = sorted({z + k - RAD for z in planes for k in range(TAPS)})
            got = {}
            for z in needed:
                if z < 0:
                    got[z] = ZR[it, 0, z + RAD, b, rows, :]
                elif z >= nz:
                    got[z] = ZR[it, 1, z - nz, b, rows, :]
                else:
                    got[z] = S[it, z, b, rows, :]
            most = M[it]
            for z in planes:
                blurred = kz[0] * got[z - RAD]
                for k in range(1, TAPS):
                    blurred = blurred + kz[k] * got[z + k - RAD]
                most = jnp.maximum(most, jnp.abs(blurred - 1.0))
                weight = (1.0 if it == 0 else W[z, b, rows, :]) / blurred
                W[z, b, rows, :] = weight
                if it < ITERS - 1:
                    Q[z, b + 1, rows, :] = weight * D[z, b + 1, rows, :]
            M[it] = most

    pl.semaphore_wait(barrier, gy_n - 1 + gz_n - 1)

    def ready(b, planes):
        if b < nb:
            for z in planes:
                in_copy(z, b).wait()

    ready(0, edge_planes)
    for b in range(nb):
        ready(b + 1, edge_planes)
        smear_x(D, 0, b, True)
        start(y_copy, y_has, 0, b, True)
        if b >= 1:
            arrived(y_copy, y_has, 0, b - 1, True)
            smear_y(0, b - 1, True)
            start(z_copy, z_has, 0, b - 1)
    for b in range(nb):
        ready(b, inner_planes)
    for b in range(nb):
        smear_x(D, 0, b, False)
        if b == 0:
            arrived(y_copy, y_has, 0, nb - 1, True)
            smear_y(0, nb - 1, True)
            start(z_copy, z_has, 0, nb - 1)
    start(y_copy, y_has, 0, 0, False)

    for it in range(ITERS):
        last = it == ITERS - 1
        arrived(y_copy, y_has, it, 0, False)
        for b in range(nb):
            smear_y(it, b, False)
        for b in range(nb):
            smear_z(it, b, inner_planes)
            if last:
                for z in inner_planes:
                    out_copy(z, b).start()
        if not last:
            for b in range(nb):
                smear_x(Q, it + 1, b, False)
            start(y_copy, y_has, it + 1, 0, False)
        for b in range(nb):
            arrived(z_copy, z_has, it, b)
            smear_z(it, b, edge_planes)
            if last:
                for z in edge_planes:
                    out_copy(z, b).start()
                continue
            if b >= 1:
                smear_x(Q, it + 1, b - 1, True)
                start(y_copy, y_has, it + 1, b - 1, True)
            if b >= 2:
                arrived(y_copy, y_has, it + 1, b - 2, True)
                smear_y(it + 1, b - 2, True)
                start(z_copy, z_has, it + 1, b - 2)
        if not last:
            smear_x(Q, it + 1, nb - 1, True)
            start(y_copy, y_has, it + 1, nb - 1, True)
            for b in (nb - 2, nb - 1):
                arrived(y_copy, y_has, it + 1, b, True)
                smear_y(it + 1, b, True)
                start(z_copy, z_has, it + 1, b)

    def c_copy(axis, me, count, off):
        src, dst, ss, rs = (CS.at[0], CR1, cs1, cr1) if axis == "gy" else (CS.at[1], CR2, cs2, cr2)
        return pltpu.make_async_remote_copy(
            src_ref=src, dst_ref=dst.at[off], send_sem=ss.at[off], recv_sem=rs.at[off],
            device_id={axis: lax.rem(me + off, count)},
        )

    for it in range(ITERS):
        CS[0, it:it + 1] = jnp.max(M[it], axis=0, keepdims=True)
    for off in range(1, gy_n):
        c_copy("gy", gy, gy_n, off).start()
    most = CS[0]
    for off in range(1, gy_n):
        c_copy("gy", gy, gy_n, off).wait_recv()
        most = jnp.maximum(most, CR1[off])
    CS[1] = most
    for off in range(1, gz_n):
        c_copy("gz", gz, gz_n, off).start()
    for off in range(1, gz_n):
        c_copy("gz", gz, gz_n, off).wait_recv()
        most = jnp.maximum(most, CR2[off])
    for it in range(ITERS):
        c_ref[it] = jnp.max(most[it:it + 1])

    for it in range(ITERS):
        for b in range(nb):
            sent(y_copy, y_has, it, b, True)
            sent(z_copy, z_has, it, b)
        sent(y_copy, y_has, it, 0, False)
    for off in range(1, gy_n):
        c_copy("gy", gy, gy_n, off).wait_send()
    for off in range(1, gz_n):
        c_copy("gz", gz, gz_n, off).wait_send()
    for z in inner_planes + edge_planes:
        for b in range(nb):
            out_copy(z, b).wait()


def shards(data_weight, blob_taps):
    ny, nz, xlen = data_weight.shape
    nb = xlen // LANES
    n_in = nz - 2 * RAD
    gy_n, gz_n = lax.axis_size("gy"), lax.axis_size("gz")
    f32, vmem, dma = jnp.float32, pltpu.VMEM, pltpu.SemaphoreType.DMA
    return pl.pallas_call(
        body,
        out_shape=(
            jax.ShapeDtypeStruct(data_weight.shape, f32),
            jax.ShapeDtypeStruct((ITERS,), f32),
        ),
        in_specs=[
            pl.BlockSpec(memory_space=pltpu.SMEM),
            pl.BlockSpec(memory_space=pl.ANY),
        ],
        out_specs=(
            pl.BlockSpec(memory_space=pl.ANY),
            pl.BlockSpec(memory_space=pltpu.SMEM),
        ),
        scratch_shapes=[
            vmem((nz, nb + 2, ny, LANES), f32),
            vmem((nz, nb, ny, LANES), f32),
            vmem((nz, nb + 2, ny, LANES), f32),
            vmem((nz, nb, ny + 2 * PAD, LANES), f32),
            vmem((ITERS, nz, nb, ny, LANES), f32),
            vmem((ITERS, 2, RAD, nb, ny, LANES), f32),
            vmem((ITERS, 2, nb, 2 * RAD, RAD, LANES), f32),
            vmem((ITERS, 2, nb, 2 * RAD, RAD, LANES), f32),
            vmem((ITERS, 2, nb, n_in, RAD, LANES), f32),
            vmem((ITERS, 2, nb, n_in, RAD, LANES), f32),
            vmem((ITERS, 8, LANES), f32),
            vmem((2, 8, LANES), f32),
            vmem((gy_n, 8, LANES), f32),
            vmem((gz_n, 8, LANES), f32),
            dma((nz, nb)),
            dma((nz, nb)),
            dma((ITERS, 2, nb)),
            dma((ITERS, 2, nb)),
            dma((ITERS, 2, nb)),
            dma((ITERS, 2, nb)),
            dma((ITERS, 2)),
            dma((ITERS, 2)),
            dma((gy_n,)),
            dma((gy_n,)),
            dma((gz_n,)),
            dma((gz_n,)),
        ],
        compiler_params=pltpu.CompilerParams(
            collective_id=0, has_side_effects=True, vmem_limit_bytes=62 * 1024 * 1024
        ),
        name="gridding",
    )(blob_taps, data_weight)


def solution(mesh):
    return jax.shard_map(
        shards,
        mesh=mesh,
        in_specs=(P("gy", "gz", None), P()),
        out_specs=(P("gy", "gz", None), P()),
        check_vma=False,
    )
```

time: 280 us -> 107 us (0.38)
  other arithmetic: 151 us -> 0 us
  Pallas kernels: 0 us -> 94.9 us
  blocking collectives: 45.7 us -> 0 us
  starting transfers between devices: 45 us -> 0 us
  waiting for transfers between devices: 32.6 us -> 0 us
  local copies, waits for them, and re-layouts: 3.7 us -> 11.4 us
    pallas_call x0 -> x1, Pallas kernels: none -> 94.9 us  [shards(): pl.pallas_call(body, out_shape=(jax.ShapeDtypeStruct(data_weight.shape, f...]
    add x6 -> x0, other arithmetic: 88 us -> none  [smear_valid(): result + kernel[offset] * lax.slice_in_dim(padded, offset, offset + lengt...]
    pmax x1 -> x0, blocking collectives: 45.7 us -> none  [shards(): changes.append(lax.pmax(deviation, ('gy', 'gz')))]
    reduce_max x3 -> x0, other arithmetic: 45.7 us -> none  [shards(): deviation = jnp.max(jnp.abs(blurred - 1.0))]
    ppermute x12 -> x0, starting transfers between devices: 45 us -> none  [the longest x6 37 us: with_halo(): lax.ppermute(tail, axis, [(i, (i + 1) % count) for i in range(ends)])]
    ppermute x12 -> x0, waiting for transfers between devices: 32.6 us -> none  [the longest x6 25 us: with_halo(): lax.ppermute(head, axis, [((i + 1) % count, i) for i in range(ends)])]
    mul x2 -> x0, other arithmetic: 8.77 us -> none  [shards(): product = weight * data_weight]
    div x2 -> x0, other arithmetic: 5.44 us -> none  [the longest x1 4.68 us: shards(): weight = weight / blurred]
  transfers between devices with their start and end apart: 12 -> 0, of which waited for: 11 -> 0; matrix products, arithmetic and copies ran while one was open for 0% -> 0% of each run, Pallas kernels for 0% -> 0%
where the time goes in v1:
time: 107 us
  Pallas kernels  94.9 us (89%)
  local copies, waits for them, and re-layouts  11.4 us (11%)
    pallas_call x1, Pallas kernels, shards(): pl.pallas_call(body, out_shape=(jax.ShapeDtypeStruct(data_weight.shape, f...  94.9 us
    unnamed x4, local copies, waits for them, and re-layouts  6.23 us
    pallas_call x1, local copies, waits for them, and re-layouts, shards(): pl.pallas_call(body, out_shape=(jax.ShapeDtypeStruct(data_weight.shape, f...  5.16 us

profile of v1, /device:TPU:0, one launch (start us, length us, event | category | flops | bytes accessed | tf_op | source)
XLA Modules:
  0.0 106.9 jit_solution(15016063867362037807)
XLA Ops:
  0.6 5.7 %copy.4.d_hbm = f32[80,20,640]{2,1,0:T(8,128)} copy(f32[80,20,640]{2,0,1:T(8,128)} %param.2) | data formatting | bytes 8192000 | tf_op args[0]
  6.3 94.9 %gridding.1 = (f32[80,20,640]{2,1,0:T(8,128)}, f32[3]{0:T(128)}) custom-call(f32[3,7]{1,0:T(4,128)} %taps_ref.1, f32[80,20,640]{2,1,0:T(8,128)} %copy.4.d_hbm), custom_call_target="tpu_custom_call" | custom-call | tf_op jit(solution)/shard_map/gridding/pallas_call | solution.py:311
  101.2 0.0 copy-start
  101.2 5.2 %copy.5 = f32[80,20,640]{2,0,1:T(8,128)} copy(f32[80,20,640]{2,1,0:T(8,128)} %get-tuple-element.2) | data formatting | bytes 8192000 | tf_op jit(solution)/shard_map/gridding/pallas_call | solution.py:311
  106.4 0.0 copy-done
  106.4 0.5 copy.7
Async XLA Ops:
  101.2 5.2 %copy-start = (f32[3]{0:T(128)S(1)}, f32[3]{0:T(128)}, u32[]{:S(2)}) copy-start(f32[3]{0:T(128)} %get-tuple-element.7) | copy-start | bytes 40

commit v2 on v1

--- a/solution.py
+++ b/solution.py
@@ -16,10 +16,10 @@
 
 def body(
     taps_ref, d_hbm, o_hbm, c_ref,
-    D, W, Q, T, S, ZR, YSB, YRB, YSI, YRI, M, CS, CR1, CR2,
+    KX, D, W, Q, T, S, ZR, YSB, YRB, YSI, YRI, M, CS, CR1, CR2,
     in_sem, out_sem, zs, zr, ysb, yrb, ysi, yri, cs1, cr1, cs2, cr2,
 ):
-    ny, nz, xlen = d_hbm.shape
+    nz, ny, xlen = d_hbm.shape
     nb = xlen // LANES
     n_in = nz - 2 * RAD
     gy_n, gz_n = lax.axis_size("gy"), lax.axis_size("gz")
@@ -39,12 +39,12 @@
 
     def in_copy(z, b):
         return pltpu.make_async_copy(
-            d_hbm.at[:, z, pl.ds(b * LANES, LANES)], D.at[z, b + 1], in_sem.at[z, b]
+            d_hbm.at[z, :, pl.ds(b * LANES, LANES)], D.at[z, b + 1], in_sem.at[z, b]
         )
 
     def out_copy(z, b):
         return pltpu.make_async_copy(
-            W.at[z, b], o_hbm.at[:, z, pl.ds(b * LANES, LANES)], out_sem.at[z, b]
+            W.at[z, b], o_hbm.at[z, :, pl.ds(b * LANES, LANES)], out_sem.at[z, b]
         )
 
     for b in range(nb):
@@ -91,33 +91,53 @@
     def wide(tap, rows):
         return tap if rows == 8 else jnp.concatenate([tap] * (rows // 8), axis=0)
 
-    lane = lax.broadcasted_iota(jnp.int32, (step, LANES), 1)
+    row = lax.broadcasted_iota(jnp.int32, (LANES, LANES), 0)
+    gap = row - lax.broadcasted_iota(jnp.int32, (LANES, LANES), 1)
+    for part in range(2):
+        taps = jnp.zeros((LANES, LANES), jnp.float32)
+        for k in range(TAPS):
+            tap = wide(taps_x[k], LANES)
+            if part == 0:
+                taps = jnp.where(gap == k - RAD, tap, taps)
+            elif k < RAD:
+                taps = jnp.where(gap == k - RAD + LANES, tap, taps)
+            elif k > RAD:
+                taps = jnp.where(gap == k - RAD - LANES, tap, taps)
+        large = taps.astype(jnp.bfloat16)
+        small = (taps - large.astype(jnp.float32)).astype(jnp.bfloat16)
+        both = jnp.concatenate([large, small], axis=1)
+        KX[pl.ds(part * LANES, LANES), :] = both
+        KX[pl.ds((2 + part) * LANES, LANES), :] = both
+
+    near = lax.broadcasted_iota(jnp.int32, (ny, LANES), 1) < LANES // 2
 
     def plane_of(i):
         return i + (i // RAD) * n_in
 
     def smear_x(src, it, b, edge):
-        kx = [wide(t, step) for t in taps_x]
-
-        @pl.loop(0, 2 * RAD if edge else n_in)
-        def _(i):
-            z = plane_of(i) if edge else i + RAD
-            for r in range(0, ny, step):
-                rows = pl.ds(r, step)
-                mid = src[z, b + 1, rows, :]
-                left = src[z, b, rows, :]
-                right = src[z, b + 2, rows, :]
-                total = kx[RAD] * mid
-                for s in range(1, RAD + 1):
-                    up = pltpu.roll(jnp.where(lane < s, right, mid), LANES - s, 1)
-                    down = pltpu.roll(jnp.where(lane >= LANES - s, left, mid), s, 1)
-                    total = total + kx[RAD + s] * up + kx[RAD - s] * down
-                T[z, b, pl.ds(PAD + r, step), :] = total
-                send = YSB if edge else YSI
-                if r == 0:
-                    send[it, 0, b, i] = total[:RAD]
-                if r + step == ny:
-                    send[it, 1, b, i] = total[step - RAD:]
+        send = YSB if edge else YSI
+        group = RAD if edge else (7 if n_in % 7 == 0 else 1)
+
+        @pl.loop(0, (2 * RAD if edge else n_in) // group)
+        def _(step_at):
+            first = step_at * (n_in + RAD) if edge else RAD + step_at * group
+            rows = []
+            for g in range(group):
+                z = first + g
+                fringe = jnp.where(near, src[z, b + 2], src[z, b])
+                cells = jnp.concatenate([src[z, b + 1], fringe], axis=1)
+                large = cells.astype(jnp.bfloat16)
+                small = (cells - large.astype(jnp.float32)).astype(jnp.bfloat16)
+                rows.append(jnp.concatenate([large, small], axis=1))
+            made = jnp.dot(
+                jnp.concatenate(rows, axis=0), KX[...], preferred_element_type=jnp.float32
+            )
+            total = made[:, :LANES] + made[:, LANES:]
+            for g in range(group):
+                plane = total[g * ny:(g + 1) * ny]
+                T[first + g, b, pl.ds(PAD, ny), :] = plane
+                send[it, 0, b, step_at * group + g] = plane[:RAD]
+                send[it, 1, b, step_at * group + g] = plane[ny - RAD:]
 
     def y_copy(it, to, b, edge):
         if edge:
@@ -308,10 +328,10 @@
     n_in = nz - 2 * RAD
     gy_n, gz_n = lax.axis_size("gy"), lax.axis_size("gz")
     f32, vmem, dma = jnp.float32, pltpu.VMEM, pltpu.SemaphoreType.DMA
-    return pl.pallas_call(
+    weight, changes = pl.pallas_call(
         body,
         out_shape=(
-            jax.ShapeDtypeStruct(data_weight.shape, f32),
+            jax.ShapeDtypeStruct((nz, ny, xlen), f32),
             jax.ShapeDtypeStruct((ITERS,), f32),
         ),
         in_specs=[
@@ -323,6 +343,7 @@
             pl.BlockSpec(memory_space=pltpu.SMEM),
         ),
         scratch_shapes=[
+            vmem((4 * LANES, 2 * LANES), jnp.bfloat16),
             vmem((nz, nb + 2, ny, LANES), f32),
             vmem((nz, nb, ny, LANES), f32),
             vmem((nz, nb + 2, ny, LANES), f32),
@@ -354,7 +375,8 @@
             collective_id=0, has_side_effects=True, vmem_limit_bytes=62 * 1024 * 1024
         ),
         name="gridding",
-    )(blob_taps, data_weight)
+    )(blob_taps, jnp.transpose(data_weight, (1, 0, 2)))
+    return jnp.transpose(weight, (1, 0, 2)), changes
 
 
 def solution(mesh):

time: 107 us -> 80.5 us (0.75)
  Pallas kernels: 94.9 us -> 74.8 us
  local copies, waits for them, and re-layouts: 11.4 us -> 4.92 us
    pallas_call x1, Pallas kernels: 94.9 us -> 74.8 us  [shards(): pl.pallas_call(body, out_shape=(jax.ShapeDtypeStruct((nz, ny, xlen), f32)...]
    pallas_call x1 -> x0, local copies, waits for them, and re-layouts: 5.16 us -> none  [shards(): pl.pallas_call(body, out_shape=(jax.ShapeDtypeStruct(data_weight.shape, f...]
    unnamed x4, local copies, waits for them, and re-layouts: 6.23 us -> 4.92 us
where the time goes in v2:
time: 80.5 us; the launch traced here: 80.4 us
  Pallas kernels  74.8 us (93%)
  local copies, waits for them, and re-layouts  4.92 us (6%)
    pallas_call x1, Pallas kernels, shards(): pl.pallas_call(body, out_shape=(jax.ShapeDtypeStruct((nz, ny, xlen), f32)...  74.8 us
    unnamed x4, local copies, waits for them, and re-layouts  4.92 us

profile of v2, /device:TPU:0, one launch (start us, length us, event | category | flops | bytes accessed | tf_op | source)
XLA Modules:
  0.0 80.4 jit_solution(15873204951943113798)
XLA Ops:
  0.6 74.8 %gridding.1 = (f32[20,80,640]{2,1,0:T(8,128)}, f32[3]{0:T(128)}) custom-call(f32[3,7]{1,0:T(4,128)} %taps_ref.1, f32[20,80,640]{2,1,0:T(8,128)} %bitcast.2), custom_call_target="tpu_custom_call" | custom-call | tf_op jit(solution)/shard_map/gridding/pallas_call | solution.py:331
  75.4 0.0 copy-start
  75.4 4.4 %copy.6 = f32[80,20,640]{2,0,1:T(8,128)} copy(f32[80,20,640]{2,0,1:T(8,128)} %bitcast.3) | data formatting | bytes 8192000
  79.8 0.0 copy-done
  79.9 0.5 copy.7
Async XLA Ops:
  75.4 4.4 %copy-start = (f32[3]{0:T(128)S(1)}, f32[3]{0:T(128)}, u32[]{:S(2)}) copy-start(f32[3]{0:T(128)} %get-tuple-element.9) | copy-start | bytes 40
